TPU v7x, 32 devices: a whole 2x2x4 slice. The times are simulated.
32 devices in a mesh: tm: 4 (over y, x), row: 4 (over z), col: 2 (over core).
Axes of the slice: x: 2, y: 2, z: 4, core: 2. Of those that a mesh axis runs over, the one named last changes fastest.
Arguments:
- noisy_video: float32 [16, 512, 512], P('tm', 'row', 'col'), may hold values from -6 to 6
- fidelity: float32 [16, 512, 512], P('tm', 'row', 'col'), may hold values from 0.5 to 12, as said below
Outputs:
- denoised: float32 [16, 512, 512], P('tm', 'row', 'col')
- gaps: float32 [3], replicated
Inputs may be any that keep to these rules, and one draw needn't show every extreme that they name: `fidelity`: positive, larger on average toward later rows.
All inputs are finite; a program needn't handle non-finite values.
Results may differ from a plain program's by a relative error of at most 0.0001.
Values sent between devices are 32-bit elements; how exact they have to be, the bound alone decides.
A program may use at most 64 MiB of HBM per device.

v0:
```python
import functools

import jax
import jax.numpy as jnp
from jax import lax
from jax.experimental import pallas as pl
from jax.experimental.pallas import tpu as pltpu
from jax.sharding import PartitionSpec as P

ITERS = 3
SIGMA = 0.28
TAU = 0.28
MESH = pl.DeviceIdType.MESH

ROW_TO = ((0, -1, 0), (0, 1, 0), (1, -1, 0), (-1, 1, 0))
COL_TO = ((0, 0, -1), (0, 0, 1), (1, 0, -1), (-1, 0, 1), (0, 1, -1), (0, -1, 1))
FRAME_TO = ((-1, 0, 0), (1, 0, 0))


def kernel(
    sizes, groups, f_hbm, lam_hbm, out_hbm, gaps_ref,
    ub, lam, inv_lam, inv_den, uus, p0s, p1s, p2s, gus, es,
    pr, pc, hc, mp, sr, sc, rsr, rsc, gsend, grecv,
    ld_sem, out_sem, fs_sem, fr_sem, rs_sem, rr_sem, cs_sem, cr_sem, gs_sem, gr_sem,
):
    nt, nr, nc = sizes
    n = nt * nr * nc
    frames, rows, cols = f_hbm.shape
    it, ir, ic = lax.axis_index("tm"), lax.axis_index("row"), lax.axis_index("col")
    me = (it * nr + ir) * nc + ic
    per = rows // groups
    chunks = per // 8
    half = cols // 128
    f32 = jnp.float32

    def exists(off):
        cond = None
        for pos, size, d in zip((it, ir, ic), sizes, off):
            if d:
                c = pos + d < size if d > 0 else pos > 0
                cond = c if cond is None else jnp.logical_and(cond, c)
        return cond

    def place(off):
        return tuple(
            jnp.clip(pos + d, 0, size - 1) if d else pos
            for pos, size, d in zip((it, ir, ic), sizes, off)
        )

    def device(index):
        return (index // (nr * nc), (index // nc) % nr, index % nc)

    load_f = [
        pltpu.make_async_copy(
            f_hbm.at[t], ub[0].at[t + 1, pl.ds(0, rows), pl.ds(0, cols)], ld_sem.at[t]
        )
        for t in range(frames)
    ]
    load_lam = pltpu.make_async_copy(lam_hbm, lam, ld_sem.at[frames])
    for t in (0, frames - 1, *range(1, frames - 1)):
        load_f[t].start()
    load_lam.start()

    barrier = pltpu.get_barrier_semaphore()

    def greet(j, carry):
        pl.semaphore_signal(
            barrier, inc=1, device_id=device((me + j) % n), device_id_type=MESH
        )
        return carry

    lax.fori_loop(1, n, greet, 0)

    def row_copy(k, i):
        return pltpu.make_async_remote_copy(
            sr.at[k], rsr.at[k, i], rs_sem.at[k, i], rr_sem.at[k, i],
            device_id=place(ROW_TO[i]), device_id_type=MESH,
        )

    def col_copy(k, i):
        return pltpu.make_async_remote_copy(
            sc.at[k], rsc.at[k, i], cs_sem.at[k, i], cr_sem.at[k, i],
            device_id=place(COL_TO[i]), device_id_type=MESH,
        )

    def frame_copy(k, i, g):
        src_frame, dst_frame = ((1, frames + 1), (frames, 0))[i]
        part = pl.ds(pl.multiple_of(g * per, 8), per)
        return pltpu.make_async_remote_copy(
            ub[k].at[src_frame, part, pl.ds(0, cols)],
            ub[k].at[dst_frame, part, pl.ds(0, cols)],
            fs_sem.at[k, i, g], fr_sem.at[k, i, g],
            device_id=place(FRAME_TO[i]), device_id_type=MESH,
        )

    def back(off):
        return tuple(-d for d in off)

    def send_frames(k, g):
        for i in (0, 1):
            @pl.when(exists(FRAME_TO[i]))
            def _(i=i):
                frame_copy(k, i, g).start()

    def wait_frames(k, g):
        for i in (0, 1):
            @pl.when(exists(back(FRAME_TO[i])))
            def _(i=i):
                frame_copy(k, i, g).wait_recv()

    def send_small(k):
        for t in range(frames):
            sr[k, t : t + 1, :] = ub[k][t + 1, 0:1, 0:cols]
            sr[k, frames + t : frames + t + 1, :] = ub[k][t + 1, rows - 1 : rows, 0:cols]
        for i in range(len(ROW_TO)):
            @pl.when(exists(ROW_TO[i]))
            def _(i=i):
                row_copy(k, i).start()
        sc[k] = mp[...].T[0:8, :]
        for i in range(len(COL_TO)):
            @pl.when(exists(COL_TO[i]))
            def _(i=i):
                col_copy(k, i).start()

    def wait_small(k):
        for i in range(len(ROW_TO)):
            @pl.when(exists(back(ROW_TO[i])))
            def _(i=i):
                row_copy(k, i).wait_recv()
        for i in range(len(COL_TO)):
            @pl.when(exists(back(COL_TO[i])))
            def _(i=i):
                col_copy(k, i).wait_recv()

    lane = lax.broadcasted_iota(jnp.int32, (8, 128), 1)
    sub = lax.broadcasted_iota(jnp.int32, (8, 128), 0)
    lane_w = lax.broadcasted_iota(jnp.int32, (8, cols), 1)
    sub_w = lax.broadcasted_iota(jnp.int32, (8, cols), 0)
    end_t, end_r, end_c = it == nt - 1, ir == nr - 1, ic == nc - 1

    def pack_cols(firsts, lasts):
        packed = jnp.zeros((8, 128), f32)
        for t in range(frames):
            packed = jnp.where(lane == t, pltpu.roll(firsts[t], t, 1) if t else firsts[t], packed)
            packed = jnp.where(lane == frames + t, pltpu.roll(lasts[t], frames + t + 1, 1), packed)
        return packed

    for c in load_f:
        c.wait()

    def first_pack(c, carry):
        r = pl.ds(pl.multiple_of(c * 8, 8), 8)
        mp[r, :] = pack_cols(
            [ub[0][t + 1, r, 0:128] for t in range(frames)],
            [ub[0][t + 1, r, cols - 128 : cols] for t in range(frames)],
        )
        return carry

    lax.fori_loop(0, rows // 8, first_pack, 0)
    pl.semaphore_wait(barrier, n - 1)
    send_small(0)
    for g in range(groups):
        send_frames(0, g)
    load_lam.wait()

    def prepare(c, carry):
        r = pl.ds(pl.multiple_of(c * 8, 8), 8)
        for t in range(frames):
            value = lam[t, r, :]
            inv_lam[t, r, :] = 0.5 / value
            inv_den[t, r, :] = 1.0 / (1.0 + TAU * value)
        return carry

    lax.fori_loop(0, rows // 8, prepare, 0)

    def shrink(m):
        s = jnp.minimum(1.0, lax.rsqrt(m[0] * m[0] + m[1] * m[1] + m[2] * m[2]))
        return [v * s for v in m]

    def edge_duals(k):
        a = rsr[k, 1]
        ahead_t = jnp.where(sub_w == 7, pltpu.roll(rsr[k, 3], 3, 0), pltpu.roll(a, 7, 0))
        corner = pltpu.roll(rsc[k, 4], 4, 0)[:, 127:128]
        ahead_c = jnp.where(lane_w == cols - 1, corner, pltpu.roll(a, cols - 1, 1))
        g = [
            jnp.where(jnp.logical_and(sub_w == 7, end_t), 0.0, ahead_t - a),
            pltpu.roll(sr[k], 4, 0) - a,
            jnp.where(jnp.logical_and(lane_w == cols - 1, end_c), 0.0, ahead_c - a),
        ]
        m = [SIGMA * v if k == 0 else pr[d] + SIGMA * v for d, v in enumerate(g)]
        m = shrink(m)
        for d in range(3):
            pr[d] = m[d]
        above = jnp.where(ir > 0, m[1], 0.0)
        for t in range(frames):
            p1s[k][t + 1][7:8, :] = above[frames + t : frames + t + 1, :]
        b = rsc[k, 1]
        ahead_t = jnp.where(sub == 7, pltpu.roll(rsc[k, 3], 3, 0), pltpu.roll(b, 7, 0))
        corner = rsc[k, 5][:, 0:1]
        ahead_r = jnp.where(lane == 127, corner, pltpu.roll(b, 127, 1))
        g = [
            jnp.where(jnp.logical_and(sub == 7, end_t), 0.0, ahead_t - b),
            jnp.where(jnp.logical_and(lane == 127, end_r), 0.0, ahead_r - b),
            pltpu.roll(sc[k], 4, 0) - b,
        ]
        m = [SIGMA * v if k == 0 else pc[d] + SIGMA * v for d, v in enumerate(g)]
        m = shrink(m)
        for d in range(3):
            pc[d] = m[d]
        left = jnp.where(ic > 0, m[2], 0.0)
        right = jnp.where(sub == frames, pltpu.roll(rsc[k, 2], 1, 0), rsc[k, 0])
        hc[...] = jnp.concatenate(
            [right, left, jnp.zeros((112, 128), f32)], axis=0
        ).T
        for t in range(frames):
            ub[k][t + 1, rows : rows + 1, 0:cols] = rsr[k, 0, t : t + 1, :]
        ub[k][0, rows : rows + 1, 0:cols] = rsr[k, 2, frames - 1 : frames, :]

    def lanes(h):
        return pl.ds(h * 128, 128)

    def gap_term(g, e, noisy, inv, weight, u):
        term = jnp.sqrt(g[0] * g[0] + g[1] * g[1] + g[2] * g[2]) + e * (e * inv + noisy)
        if u is None:
            return term
        resid = u - noisy
        return term + 0.5 * weight * resid * resid

    def chunk(k, c, acc):
        r0 = pl.multiple_of(c * 8, 8)
        r = pl.ds(r0, 8)
        below = pl.ds(pl.multiple_of(r0 + 8, 8), 8)
        last_chunk_row = jnp.logical_and(jnp.logical_and(sub == 7, end_r), c == rows // 8 - 1)
        last_lane = jnp.logical_and(lane == 127, end_c)
        halo = hc[r, :]
        prev0 = None
        firsts, lasts = [], []
        x = [ub[k][0, r, lanes(h)] for h in range(half)]
        for j in range(frames + 1):
            t = j - 1
            xn = [ub[k][j + 1, r, lanes(h)] for h in range(half)]
            where_right = t if t >= 0 else frames
            right = jnp.broadcast_to(halo[:, where_right : where_right + 1], (8, 128))
            cur0, cur2 = [], []
            if t >= 0:
                prev1 = [p1s[k][j][r, lanes(h)] for h in range(half)]
            for h in range(half):
                g0 = xn[h] - x[h]
                if t == frames - 1:
                    g0 = jnp.where(end_t, 0.0, g0)
                g1 = pltpu.roll(jnp.where(sub == 0, ub[k][j, below, lanes(h)], x[h]), 7, 0) - x[h]
                g1 = jnp.where(last_chunk_row, 0.0, g1)
                follow = x[h + 1] if h + 1 < half else right
                g2 = pltpu.roll(jnp.where(lane == 0, follow, x[h]), 127, 1) - x[h]
                if h == half - 1:
                    g2 = jnp.where(last_lane, 0.0, g2)
                g = [g0, g1, g2]
                if k == 0:
                    m = [SIGMA * v for v in g]
                else:
                    m = [
                        p0s[k - 1][j, r, lanes(h)],
                        p1s[k - 1][j][below, lanes(h)],
                        p2s[k - 1][j, r, lanes(h)],
                    ]
                    m = [q + SIGMA * v for q, v in zip(m, g)]
                m = shrink(m)
                if k < ITERS - 1:
                    p0s[k][j, r, lanes(h)] = m[0]
                    p2s[k][j, r, lanes(h)] = m[2]
                p1s[k][j][below, lanes(h)] = m[1]
                cur0.append(m[0])
                cur2.append(m[2])
                if t < 0:
                    continue
                d0 = m[0] - prev0[h]
                d1 = m[1] - pltpu.roll(jnp.where(sub == 7, prev1[h], m[1]), 1, 0)
                if h == 0:
                    before = jnp.broadcast_to(halo[:, 8 + frames + t : 9 + frames + t], (8, 128))
                else:
                    before = cur2[h - 1]
                d2 = m[2] - pltpu.roll(jnp.where(lane == 127, before, m[2]), 1, 1)
                e = d0 + d1 + d2
                if k > 0:
                    g = [0.5 * (v + gus[k - 1][d][t, r, lanes(h)]) for d, v in enumerate(g)]
                if k < ITERS - 1:
                    for d in range(3):
                        gus[k][d][t, r, lanes(h)] = g[d]
                noisy = ub[0][j, r, lanes(h)]
                weight = lam[t, r, lanes(h)]
                u = noisy if k == 0 else uus[k - 1][t, r, lanes(h)]
                if k < ITERS - 1:
                    es[t, r, lanes(h)] = e
                else:
                    acc = acc + gap_term(g, e, noisy, inv_lam[t, r, lanes(h)], weight, u)
                new = (u + TAU * e + TAU * weight * noisy) * inv_den[t, r, lanes(h)]
                uus[k][t, r, lanes(h)] = new
                if k < ITERS - 1:
                    ubar = 2.0 * new - u
                    ub[k + 1][j, r, lanes(h)] = ubar
                    if h == 0:
                        firsts.append(ubar)
                    if h == half - 1:
                        lasts.append(ubar)
            if t < 0:
                prev0 = [jnp.where(it > 0, v, 0.0) for v in cur0]
            else:
                prev0 = cur0
            x = xn
        if k < ITERS - 1:
            mp[r, :] = pack_cols(firsts, lasts)
        return acc

    def out_copy(g):
        part = pl.ds(pl.multiple_of(g * per, 8), per)
        return pltpu.make_async_copy(
            uus[ITERS - 1].at[:, part, :], out_hbm.at[:, part, :], out_sem.at[g]
        )

    def gap_chunk(k, c, acc):
        r = pl.ds(pl.multiple_of(c * 8, 8), 8)
        for t in range(frames):
            for h in range(half):
                at = (t, r, lanes(h))
                noisy = ub[0][t + 1, r, lanes(h)]
                acc = acc + gap_term(
                    [gus[k][d][at] for d in range(3)], es[at], noisy, inv_lam[at],
                    lam[at] if k else None, uus[k - 1][at] if k else None,
                )
        return acc

    local = jnp.zeros((1, 128), f32)
    lane_row = lax.broadcasted_iota(jnp.int32, (1, 128), 1)
    for k in range(ITERS):
        wait_small(k)
        edge_duals(k)
        wait_frames(k, 0)

        def group(g, acc, k=k):
            @pl.when(g + 1 < groups)
            def _():
                wait_frames(k, g + 1)

            acc = lax.fori_loop(
                0, chunks, lambda c, a: chunk(k, g * chunks + c, a), acc, unroll=4
            )
            if k < ITERS - 1:
                @pl.when(g < 1)
                def _():
                    send_frames(k + 1, g)
            else:
                out_copy(g).start()
            return acc

        acc = lax.fori_loop(0, groups, group, jnp.zeros((8, 128), f32))
        if k < ITERS - 1:
            send_small(k + 1)
            for g in range(1, groups):
                send_frames(k + 1, g)
            acc = lax.fori_loop(
                0, rows // 8, functools.partial(gap_chunk, k), acc, unroll=2
            )
        total = jnp.sum(jnp.sum(acc, axis=0, keepdims=True), axis=1, keepdims=True)
        local = jnp.where(lane_row == k, total, local)

    gsend[0] = local

    def gap_copy(j):
        return pltpu.make_async_remote_copy(
            gsend.at[0], grecv.at[j - 1], gs_sem, gr_sem,
            device_id=device((me + j) % n), device_id_type=MESH,
        )

    def tell(j, carry):
        gap_copy(j).start()
        return carry

    lax.fori_loop(1, n, tell, 0)

    for k in range(ITERS):
        for i in range(len(ROW_TO)):
            @pl.when(exists(ROW_TO[i]))
            def _(k=k, i=i):
                row_copy(k, i).wait_send()
        for i in range(len(COL_TO)):
            @pl.when(exists(COL_TO[i]))
            def _(k=k, i=i):
                col_copy(k, i).wait_send()
        for i in (0, 1):
            @pl.when(exists(FRAME_TO[i]))
            def _(k=k, i=i):
                for g in range(groups):
                    frame_copy(k, i, g).wait_send()
    for g in range(groups):
        out_copy(g).wait()
    everything = grecv.at[pl.ds(0, n - 1)]
    pltpu.make_async_copy(everything, everything, gr_sem).wait()
    pltpu.make_async_copy(everything, everything, gs_sem).wait()

    total = local + jnp.sum(grecv[...], axis=0)
    total = total * (1.0 / float(n * frames * rows * cols))
    for k in range(ITERS):
        gaps_ref[k] = jnp.sum(jnp.where(lane_row == k, total, 0.0))


def solution(mesh):
    sizes = (mesh.shape["tm"], mesh.shape["row"], mesh.shape["col"])
    n = sizes[0] * sizes[1] * sizes[2]

    def on_device(noisy_video, fidelity):
        frames, rows, cols = noisy_video.shape
        groups = 4
        block = (frames, rows, cols)
        dma = pltpu.SemaphoreType.DMA
        vm = lambda *shape: pltpu.VMEM(shape, jnp.float32)
        return pl.pallas_call(
            functools.partial(kernel, sizes, groups),
            out_shape=(
                jax.ShapeDtypeStruct(block, jnp.float32),
                jax.ShapeDtypeStruct((ITERS,), jnp.float32),
            ),
            in_specs=[pl.BlockSpec(memory_space=pltpu.HBM)] * 2,
            out_specs=(
                pl.BlockSpec(memory_space=pltpu.HBM),
                pl.BlockSpec(memory_space=pltpu.SMEM),
            ),
            scratch_shapes=[
                [vm(frames + 2, rows + 8, cols) for _ in range(ITERS)],
                vm(*block), vm(*block), vm(*block),
                [vm(*block) for _ in range(ITERS)],
                [vm(frames + 1, rows, cols) for _ in range(ITERS - 1)],
                [[vm(rows + 8, cols) for _ in range(frames + 1)] for _ in range(ITERS)],
                [vm(frames + 1, rows, cols) for _ in range(ITERS - 1)],
                [[vm(*block) for _ in range(3)] for _ in range(ITERS - 1)],
                vm(*block),
                vm(3, 8, cols), vm(3, 8, 128), vm(rows, 128), vm(rows, 128),
                vm(ITERS, 8, cols), vm(ITERS, 8, 128),
                vm(ITERS, len(ROW_TO), 8, cols), vm(ITERS, len(COL_TO), 8, 128),
                vm(1, 1, 128), vm(n - 1, 1, 128),
                dma((frames + 1,)), dma((groups,)),
                dma((ITERS, 2, groups)), dma((ITERS, 2, groups)),
                dma((ITERS, len(ROW_TO))), dma((ITERS, len(ROW_TO))),
                dma((ITERS, len(COL_TO))), dma((ITERS, len(COL_TO))),
                dma(()), dma(()),
            ],
            compiler_params=pltpu.CompilerParams(
                collective_id=0, has_side_effects=True
            ),
            name="chambolle_pock",
        )(noisy_video, fidelity)

    return jax.shard_map(
        on_device,
        mesh=mesh,
        in_specs=(P("tm", "row", "col"), P("tm", "row", "col")),
        out_specs=(P("tm", "row", "col"), P()),
        check_vma=False,
    )
```

profile of v0, /device:TPU:0, one launch (start us, length us, event | category | flops | bytes accessed | tf_op | source)
XLA Modules:
  0.0 38.2 jit_solution(6726981462319902140)
XLA Ops:
  0.6 35.1 %chambolle_pock.1 = (f32[4,128,256]{2,1,0:T(8,128)}, f32[3]{0:T(128)}) custom-call(f32[4,128,256]{2,1,0:T(8,128)} %f_hbm.1, f32[4,128,256]{2,1,0:T(8,128)} %lam_hbm.1), custom_call_target="tpu_custom_call" | custom-call | tf_op jit(solution)/shard_map/chambolle_pock/pallas_call | solution.py:416
  35.8 0.0 copy-start
  35.8 1.9 %copy.6 = f32[4,128,256]{2,1,0:T(8,128)} copy(f32[4,128,256]{2,1,0:T(8,128)} %get-tuple-element.4) | data formatting | bytes 1048576
  37.6 0.0 copy-done
  37.6 0.5 %copy.7 = f32[3]{0:T(128)} copy(f32[3]{0:T(128)S(1)} %copy-done) | data formatting | bytes 24
Async XLA Ops:
  35.8 1.9 %copy-start = (f32[3]{0:T(128)S(1)}, f32[3]{0:T(128)}, u32[]{:S(2)}) copy-start(f32[3]{0:T(128)} %get-tuple-element.5) | copy-start | bytes 40
where the time goes:
time: 38.3 us; the launch traced here: 38.2 us
  Pallas kernels  35.1 us (92%)
  local copies, waits for them, and re-layouts  2.38 us (6%)
  between operations  0.65 us (2%)
    pallas_call x1, Pallas kernels, on_device(): pl.pallas_call(functools.partial(kernel, sizes, groups), out_shape=(jax.S...  35.1 us
    unnamed x4, local copies, waits for them, and re-layouts  2.38 us

commit v1 on v0

--- a/solution.py
+++ b/solution.py
@@ -294,7 +294,7 @@
                 else:
                     acc = acc + gap_term(g, e, noisy, inv_lam[t, r, lanes(h)], weight, u)
                 new = (u + TAU * e + TAU * weight * noisy) * inv_den[t, r, lanes(h)]
-                uus[k][t, r, lanes(h)] = new
+                (out_hbm if k == ITERS - 1 else uus[k])[t, r, lanes(h)] = new
                 if k < ITERS - 1:
                     ubar = 2.0 * new - u
                     ub[k + 1][j, r, lanes(h)] = ubar
@@ -349,7 +349,7 @@
                 def _():
                     send_frames(k + 1, g)
             else:
-                out_copy(g).start()
+                pass
             return acc
 
         acc = lax.fori_loop(0, groups, group, jnp.zeros((8, 128), f32))
@@ -391,16 +391,24 @@
             def _(k=k, i=i):
                 for g in range(groups):
                     frame_copy(k, i, g).wait_send()
-    for g in range(groups):
-        out_copy(g).wait()
     everything = grecv.at[pl.ds(0, n - 1)]
     pltpu.make_async_copy(everything, everything, gr_sem).wait()
     pltpu.make_async_copy(everything, everything, gs_sem).wait()
 
     total = local + jnp.sum(grecv[...], axis=0)
     total = total * (1.0 / float(n * frames * rows * cols))
-    for k in range(ITERS):
-        gaps_ref[k] = jnp.sum(jnp.where(lane_row == k, total, 0.0))
+    gaps_ref[...] = total[0, 0:ITERS]
+
+
+def put(u, gaps, u_out, gaps_out, sem):
+    copies = [
+        pltpu.make_async_copy(u, u_out, sem.at[0]),
+        pltpu.make_async_copy(gaps, gaps_out, sem.at[1]),
+    ]
+    for c in copies:
+        c.start()
+    for c in copies:
+        c.wait()
 
 
 def solution(mesh):
@@ -413,16 +421,16 @@
         block = (frames, rows, cols)
         dma = pltpu.SemaphoreType.DMA
         vm = lambda *shape: pltpu.VMEM(shape, jnp.float32)
-        return pl.pallas_call(
+        outs = pl.pallas_call(
             functools.partial(kernel, sizes, groups),
             out_shape=(
-                jax.ShapeDtypeStruct(block, jnp.float32),
-                jax.ShapeDtypeStruct((ITERS,), jnp.float32),
+                pltpu.VMEM(block, jnp.float32),
+                pltpu.VMEM((ITERS,), jnp.float32),
             ),
             in_specs=[pl.BlockSpec(memory_space=pltpu.HBM)] * 2,
             out_specs=(
-                pl.BlockSpec(memory_space=pltpu.HBM),
-                pl.BlockSpec(memory_space=pltpu.SMEM),
+                pl.BlockSpec(memory_space=pltpu.VMEM),
+                pl.BlockSpec(memory_space=pltpu.VMEM),
             ),
             scratch_shapes=[
                 [vm(frames + 2, rows + 8, cols) for _ in range(ITERS)],
@@ -448,6 +456,17 @@
             ),
             name="chambolle_pock",
         )(noisy_video, fidelity)
+        return pl.pallas_call(
+            put,
+            out_shape=(
+                jax.ShapeDtypeStruct(block, jnp.float32),
+                jax.ShapeDtypeStruct((ITERS,), jnp.float32),
+            ),
+            in_specs=[pl.BlockSpec(memory_space=pltpu.VMEM)] * 2,
+            out_specs=[pl.BlockSpec(memory_space=pltpu.HBM)] * 2,
+            scratch_shapes=[dma((2,))],
+            name="put",
+        )(*[pltpu.with_memory_space_constraint(x, pltpu.VMEM) for x in outs])
 
     return jax.shard_map(
         on_device,

time: 38.3 us -> 36.1 us (0.943)
  local copies, waits for them, and re-layouts: 2.38 us -> 0 us
    unnamed x4 -> x0, local copies, waits for them, and re-layouts: 2.38 us -> none
    pallas_call x1 -> x2, Pallas kernels: 35.1 us -> 35.3 us  [the longest x1 34.5 us: on_device(): pl.pallas_call(functools.partial(kernel, sizes, groups), out_shape=(pltpu...]
where the time goes in v1:
time: 36.1 us; the launch traced here: 36 us
  Pallas kernels  35.3 us (98%)
  between operations  0.64 us (2%)
    pallas_call x1, Pallas kernels, on_device(): pl.pallas_call(functools.partial(kernel, sizes, groups), out_shape=(pltpu...  34.5 us
    pallas_call x1, Pallas kernels, on_device(): pl.pallas_call(put, out_shape=(jax.ShapeDtypeStruct(block, jnp.float32),...  0.81 us

profile of v1, /device:TPU:0, one launch (start us, length us, event | category | flops | bytes accessed | tf_op | source)
XLA Modules:
  0.0 36.0 jit_solution(7845977587697106116)
XLA Ops:
  0.6 34.5 %chambolle_pock.1 = (f32[4,128,256]{2,1,0:T(8,128)S(1)}, f32[3]{0:T(128)S(1)}) custom-call(f32[4,128,256]{2,1,0:T(8,128)} %f_hbm.1, f32[4,128,256]{2,1,0:T(8,128)} %lam_hbm.1), custom_call_target="tpu_custom_call" | custom-call | tf_op jit(solution)/shard_map/chambolle_pock/pallas_call | solution.py:424
  35.1 0.8 %put.1 = (f32[4,128,256]{2,1,0:T(8,128)}, f32[3]{0:T(128)}) custom-call(f32[4,128,256]{2,1,0:T(8,128)S(1)} %get-tuple-element.4.u, f32[3]{0:T(128)S(1)} %get-tuple-element.5.gaps), custom_call_target="tpu_custom_call" | custom-call | tf_op jit(solution)/shard_map/put/pallas_call | solution.py:459

commit v2 on v1

--- a/solution.py
+++ b/solution.py
@@ -21,7 +21,7 @@
     sizes, groups, f_hbm, lam_hbm, out_hbm, gaps_ref,
     ub, lam, inv_lam, inv_den, uus, p0s, p1s, p2s, gus, es,
     pr, pc, hc, mp, sr, sc, rsr, rsc, gsend, grecv,
-    ld_sem, out_sem, fs_sem, fr_sem, rs_sem, rr_sem, cs_sem, cr_sem, gs_sem, gr_sem,
+    ld_sem, fs_sem, fr_sem, rs_sem, rr_sem, cs_sem, cr_sem, gs_sem, gr_sem, hello_sem,
 ):
     nt, nr, nc = sizes
     n = nt * nr * nc
@@ -50,36 +50,74 @@
     def device(index):
         return (index // (nr * nc), (index // nc) % nr, index % nc)
 
+    def back(off):
+        return tuple(-d for d in off)
+
+    def how_many(offsets):
+        return sum(jnp.where(exists(off), 1, 0) for off in offsets)
+
+    def wait_for(count, most, sem, region):
+        for c in range(1, most + 1):
+            @pl.when(count == c)
+            def _(c=c):
+                pltpu.make_async_copy(region(c), region(c), sem).wait()
+
+    row_out, row_in = how_many(ROW_TO), how_many([back(o) for o in ROW_TO])
+    col_out, col_in = how_many(COL_TO), how_many([back(o) for o in COL_TO])
+    frame_out = how_many(FRAME_TO)
+
+    barrier = pltpu.get_barrier_semaphore()
+    near = ROW_TO + COL_TO + FRAME_TO
+    for off in near:
+        @pl.when(exists(off))
+        def _(off=off):
+            pl.semaphore_signal(
+                barrier, inc=1, device_id=place(off), device_id_type=MESH
+            )
+
     load_f = [
         pltpu.make_async_copy(
-            f_hbm.at[t], ub[0].at[t + 1, pl.ds(0, rows), pl.ds(0, cols)], ld_sem.at[t]
+            f_hbm.at[t], ub[0].at[t + 1, pl.ds(0, rows), pl.ds(0, cols)], ld_sem.at[0]
         )
         for t in range(frames)
     ]
-    load_lam = pltpu.make_async_copy(lam_hbm, lam, ld_sem.at[frames])
-    for t in (0, frames - 1, *range(1, frames - 1)):
+    load_lam = pltpu.make_async_copy(lam_hbm, lam, ld_sem.at[1])
+    for t in range(frames):
         load_f[t].start()
     load_lam.start()
 
-    barrier = pltpu.get_barrier_semaphore()
-
-    def greet(j, carry):
-        pl.semaphore_signal(
-            barrier, inc=1, device_id=device((me + j) % n), device_id_type=MESH
-        )
-        return carry
-
-    lax.fori_loop(1, n, greet, 0)
+    rounds = [1] * (nr - 2) + [2] * (nc - 1) + [0] * (nt - 1)
+
+    def hello_to(r):
+        axis = rounds[r]
+        return [tuple(d if a == axis else 0 for a in range(3)) for d in (-1, 1)]
+
+    def say_hello(r):
+        if r < len(rounds):
+            for off in hello_to(r):
+                @pl.when(exists(off))
+                def _(off=off):
+                    pl.semaphore_signal(
+                        hello_sem.at[r], inc=1, device_id=place(off), device_id_type=MESH
+                    )
+
+    def hear_hello(r):
+        if 0 <= r < len(rounds):
+            pl.semaphore_wait(hello_sem.at[r], how_many(hello_to(r)))
+
+    def next_hello(r):
+        hear_hello(r - 1)
+        say_hello(r)
 
     def row_copy(k, i):
         return pltpu.make_async_remote_copy(
-            sr.at[k], rsr.at[k, i], rs_sem.at[k, i], rr_sem.at[k, i],
+            sr.at[k], rsr.at[k, i], rs_sem.at[0], rr_sem.at[k],
             device_id=place(ROW_TO[i]), device_id_type=MESH,
         )
 
     def col_copy(k, i):
         return pltpu.make_async_remote_copy(
-            sc.at[k], rsc.at[k, i], cs_sem.at[k, i], cr_sem.at[k, i],
+            sc.at[k], rsc.at[k, i], cs_sem.at[0], cr_sem.at[k],
             device_id=place(COL_TO[i]), device_id_type=MESH,
         )
 
@@ -89,12 +127,9 @@
         return pltpu.make_async_remote_copy(
             ub[k].at[src_frame, part, pl.ds(0, cols)],
             ub[k].at[dst_frame, part, pl.ds(0, cols)],
-            fs_sem.at[k, i, g], fr_sem.at[k, i, g],
+            fs_sem.at[k], fr_sem.at[k, g],
             device_id=place(FRAME_TO[i]), device_id_type=MESH,
         )
-
-    def back(off):
-        return tuple(-d for d in off)
 
     def send_frames(k, g):
         for i in (0, 1):
@@ -103,12 +138,13 @@
                 frame_copy(k, i, g).start()
 
     def wait_frames(k, g):
-        for i in (0, 1):
-            @pl.when(exists(back(FRAME_TO[i])))
-            def _(i=i):
-                frame_copy(k, i, g).wait_recv()
-
-    def send_small(k):
+        part = pl.ds(pl.multiple_of(g * per, 8), per)
+        wait_for(
+            frame_out, 2, fr_sem.at[k, g],
+            lambda c: ub[k].at[pl.ds(0, c), part, pl.ds(0, cols)],
+        )
+
+    def send_rows(k):
         for t in range(frames):
             sr[k, t : t + 1, :] = ub[k][t + 1, 0:1, 0:cols]
             sr[k, frames + t : frames + t + 1, :] = ub[k][t + 1, rows - 1 : rows, 0:cols]
@@ -116,21 +152,21 @@
             @pl.when(exists(ROW_TO[i]))
             def _(i=i):
                 row_copy(k, i).start()
+
+    def send_cols(k):
         sc[k] = mp[...].T[0:8, :]
         for i in range(len(COL_TO)):
             @pl.when(exists(COL_TO[i]))
             def _(i=i):
                 col_copy(k, i).start()
 
+    def send_small(k):
+        send_rows(k)
+        send_cols(k)
+
     def wait_small(k):
-        for i in range(len(ROW_TO)):
-            @pl.when(exists(back(ROW_TO[i])))
-            def _(i=i):
-                row_copy(k, i).wait_recv()
-        for i in range(len(COL_TO)):
-            @pl.when(exists(back(COL_TO[i])))
-            def _(i=i):
-                col_copy(k, i).wait_recv()
+        wait_for(row_in, len(ROW_TO), rr_sem.at[k], lambda c: rsr.at[k, pl.ds(0, c)])
+        wait_for(col_in, len(COL_TO), cr_sem.at[k], lambda c: rsc.at[k, pl.ds(0, c)])
 
     lane = lax.broadcasted_iota(jnp.int32, (8, 128), 1)
     sub = lax.broadcasted_iota(jnp.int32, (8, 128), 0)
@@ -145,8 +181,8 @@
             packed = jnp.where(lane == frames + t, pltpu.roll(lasts[t], frames + t + 1, 1), packed)
         return packed
 
-    for c in load_f:
-        c.wait()
+    loaded = ub[0].at[pl.ds(1, frames), pl.ds(0, rows), pl.ds(0, cols)]
+    pltpu.make_async_copy(loaded, loaded, ld_sem.at[0]).wait()
 
     def first_pack(c, carry):
         r = pl.ds(pl.multiple_of(c * 8, 8), 8)
@@ -156,11 +192,12 @@
         )
         return carry
 
-    lax.fori_loop(0, rows // 8, first_pack, 0)
-    pl.semaphore_wait(barrier, n - 1)
+    lax.fori_loop(0, rows // 8, first_pack, 0, unroll=8)
+    pl.semaphore_wait(barrier, how_many(near))
     send_small(0)
     for g in range(groups):
         send_frames(0, g)
+    say_hello(0)
     load_lam.wait()
 
     def prepare(c, carry):
@@ -311,12 +348,6 @@
             mp[r, :] = pack_cols(firsts, lasts)
         return acc
 
-    def out_copy(g):
-        part = pl.ds(pl.multiple_of(g * per, 8), per)
-        return pltpu.make_async_copy(
-            uus[ITERS - 1].at[:, part, :], out_hbm.at[:, part, :], out_sem.at[g]
-        )
-
     def gap_chunk(k, c, acc):
         r = pl.ds(pl.multiple_of(c * 8, 8), 8)
         for t in range(frames):
@@ -334,6 +365,7 @@
     for k in range(ITERS):
         wait_small(k)
         edge_duals(k)
+        next_hello(2 * k + 1)
         wait_frames(k, 0)
 
         def group(g, acc, k=k):
@@ -348,11 +380,10 @@
                 @pl.when(g < 1)
                 def _():
                     send_frames(k + 1, g)
-            else:
-                pass
             return acc
 
         acc = lax.fori_loop(0, groups, group, jnp.zeros((8, 128), f32))
+        next_hello(2 * k + 2)
         if k < ITERS - 1:
             send_small(k + 1)
             for g in range(1, groups):
@@ -363,6 +394,9 @@
         total = jnp.sum(jnp.sum(acc, axis=0, keepdims=True), axis=1, keepdims=True)
         local = jnp.where(lane_row == k, total, local)
 
+    for r in range(2 * ITERS, len(rounds)):
+        next_hello(r + 1)
+
     gsend[0] = local
 
     def gap_copy(j):
@@ -371,26 +405,21 @@
             device_id=device((me + j) % n), device_id_type=MESH,
         )
 
-    def tell(j, carry):
-        gap_copy(j).start()
+    def tell(b, carry):
+        for c in range(spread):
+            gap_copy(b * spread + c + 1).start()
         return carry
 
-    lax.fori_loop(1, n, tell, 0)
-
+    spread = max(d for d in range(1, 33) if (n - 1) % d == 0)
+    lax.fori_loop(0, (n - 1) // spread, tell, 0)
+
+    wait_for(row_out, len(ROW_TO), rs_sem.at[0], lambda c: rsr.at[:, pl.ds(0, c)])
+    wait_for(col_out, len(COL_TO), cs_sem.at[0], lambda c: rsc.at[:, pl.ds(0, c)])
     for k in range(ITERS):
-        for i in range(len(ROW_TO)):
-            @pl.when(exists(ROW_TO[i]))
-            def _(k=k, i=i):
-                row_copy(k, i).wait_send()
-        for i in range(len(COL_TO)):
-            @pl.when(exists(COL_TO[i]))
-            def _(k=k, i=i):
-                col_copy(k, i).wait_send()
-        for i in (0, 1):
-            @pl.when(exists(FRAME_TO[i]))
-            def _(k=k, i=i):
-                for g in range(groups):
-                    frame_copy(k, i, g).wait_send()
+        wait_for(
+            frame_out, 2, fs_sem.at[k],
+            lambda c, k=k: ub[k].at[pl.ds(0, c), pl.ds(0, rows), pl.ds(0, cols)],
+        )
     everything = grecv.at[pl.ds(0, n - 1)]
     pltpu.make_async_copy(everything, everything, gr_sem).wait()
     pltpu.make_async_copy(everything, everything, gs_sem).wait()
@@ -445,11 +474,10 @@
                 vm(ITERS, 8, cols), vm(ITERS, 8, 128),
                 vm(ITERS, len(ROW_TO), 8, cols), vm(ITERS, len(COL_TO), 8, 128),
                 vm(1, 1, 128), vm(n - 1, 1, 128),
-                dma((frames + 1,)), dma((groups,)),
-                dma((ITERS, 2, groups)), dma((ITERS, 2, groups)),
-                dma((ITERS, len(ROW_TO))), dma((ITERS, len(ROW_TO))),
-                dma((ITERS, len(COL_TO))), dma((ITERS, len(COL_TO))),
+                dma((2,)), dma((ITERS,)), dma((ITERS, groups)),
+                dma((1,)), dma((ITERS,)), dma((1,)), dma((ITERS,)),
                 dma(()), dma(()),
+                pltpu.SemaphoreType.REGULAR((max(1, sum(sizes) - 4),)),
             ],
             compiler_params=pltpu.CompilerParams(
                 collective_id=0, has_side_effects=True

time: 36.1 us -> 34.3 us (0.950)
  Pallas kernels: 35.3 us -> 33.5 us
    pallas_call x1, Pallas kernels: 34.5 us -> 32.7 us  [on_device(): pl.pallas_call(functools.partial(kernel, sizes, groups), out_shape=(pltpu...]
where the time goes in v2:
time: 34.3 us; the launch traced here: 34.1 us
  Pallas kernels  33.5 us (98%)
  between operations  0.64 us (2%)
    pallas_call x1, Pallas kernels, on_device(): pl.pallas_call(functools.partial(kernel, sizes, groups), out_shape=(pltpu...  32.7 us
    pallas_call x1, Pallas kernels, on_device(): pl.pallas_call(put, out_shape=(jax.ShapeDtypeStruct(block, jnp.float32),...  0.81 us

profile of v2, /device:TPU:0, one launch (start us, length us, event | category | flops | bytes accessed | tf_op | source)
XLA Modules:
  0.0 34.1 jit_solution(4884056944603514189)
XLA Ops:
  0.6 32.7 %chambolle_pock.1 = (f32[4,128,256]{2,1,0:T(8,128)S(1)}, f32[3]{0:T(128)S(1)}) custom-call(f32[4,128,256]{2,1,0:T(8,128)} %f_hbm.1, f32[4,128,256]{2,1,0:T(8,128)} %lam_hbm.1), custom_call_target="tpu_custom_call" | custom-call | tf_op jit(solution)/shard_map/chambolle_pock/pallas_call | solution.py:453
  33.3 0.8 %put.1 = (f32[4,128,256]{2,1,0:T(8,128)}, f32[3]{0:T(128)}) custom-call(f32[4,128,256]{2,1,0:T(8,128)S(1)} %get-tuple-element.4.u, f32[3]{0:T(128)S(1)} %get-tuple-element.5.gaps), custom_call_target="tpu_custom_call" | custom-call | tf_op jit(solution)/shard_map/put/pallas_call | solution.py:487

commit v3 on v2

--- a/solution.py
+++ b/solution.py
@@ -18,10 +18,11 @@
 
 
 def kernel(
-    sizes, groups, f_hbm, lam_hbm, out_hbm, gaps_ref,
+    sizes, groups, early, relays, f_hbm, lam_hbm, out_hbm, gaps_ref,
     ub, lam, inv_lam, inv_den, uus, p0s, p1s, p2s, gus, es,
     pr, pc, hc, mp, sr, sc, rsr, rsc, gsend, grecv,
     ld_sem, fs_sem, fr_sem, rs_sem, rr_sem, cs_sem, cr_sem, gs_sem, gr_sem, hello_sem,
+    rbuf, rl_sem, fw_sem,
 ):
     nt, nr, nc = sizes
     n = nt * nr * nc
@@ -68,6 +69,16 @@
 
     barrier = pltpu.get_barrier_semaphore()
     near = ROW_TO + COL_TO + FRAME_TO
+    met = how_many(near)
+    for src, via, dst, i, slot in relays:
+        for a, b in ((src, via), (via, src)):
+            met = met + jnp.where(it == a, 1, 0)
+
+            @pl.when(it == a)
+            def _(b=b):
+                pl.semaphore_signal(
+                    barrier, inc=1, device_id=(b, ir, ic), device_id_type=MESH
+                )
     for off in near:
         @pl.when(exists(off))
         def _(off=off):
@@ -131,11 +142,45 @@
             device_id=place(FRAME_TO[i]), device_id_type=MESH,
         )
 
-    def send_frames(k, g):
+    relay_from = groups - groups // 2
+
+    def send_frames(k, g, direct=True):
         for i in (0, 1):
-            @pl.when(exists(FRAME_TO[i]))
+            there = exists(FRAME_TO[i])
+            if not direct:
+                for src, via, dst, j, slot in relays:
+                    if i == j:
+                        there = jnp.logical_and(there, it != src)
+
+            @pl.when(there)
             def _(i=i):
                 frame_copy(k, i, g).start()
+
+    def send_relay(k, g):
+        for src, via, dst, i, slot in relays:
+            @pl.when(it == src)
+            def _(via=via, i=i, slot=slot):
+                part = pl.ds(pl.multiple_of(g * per, 8), per)
+                h = g - relay_from
+                pltpu.make_async_remote_copy(
+                    ub[k].at[(1, frames)[i], part, pl.ds(0, cols)], rbuf.at[slot, k, h],
+                    fs_sem.at[k], rl_sem.at[slot, k, h],
+                    device_id=(via, ir, ic), device_id_type=MESH,
+                ).start()
+
+    def forward(k):
+        for src, via, dst, i, slot in relays:
+            @pl.when(it == via)
+            def _(dst=dst, i=i, slot=slot):
+                for g in range(relay_from, groups):
+                    box = rbuf.at[slot, k, g - relay_from]
+                    pltpu.make_async_copy(box, box, rl_sem.at[slot, k, g - relay_from]).wait()
+                    pltpu.make_async_remote_copy(
+                        box,
+                        ub[k].at[(frames + 1, 0)[i], pl.ds(g * per, per), pl.ds(0, cols)],
+                        fw_sem.at[slot], fr_sem.at[k, g],
+                        device_id=(dst, ir, ic), device_id_type=MESH,
+                    ).start()
 
     def wait_frames(k, g):
         part = pl.ds(pl.multiple_of(g * per, 8), per)
@@ -193,10 +238,13 @@
         return carry
 
     lax.fori_loop(0, rows // 8, first_pack, 0, unroll=8)
-    pl.semaphore_wait(barrier, how_many(near))
+    pl.semaphore_wait(barrier, met)
     send_small(0)
+    if relays:
+        for g in range(relay_from, groups):
+            send_relay(0, g)
     for g in range(groups):
-        send_frames(0, g)
+        send_frames(0, g, g < relay_from)
     say_hello(0)
     load_lam.wait()
 
@@ -363,6 +411,7 @@
     local = jnp.zeros((1, 128), f32)
     lane_row = lax.broadcasted_iota(jnp.int32, (1, 128), 1)
     for k in range(ITERS):
+        forward(k)
         wait_small(k)
         edge_duals(k)
         next_hello(2 * k + 1)
@@ -374,20 +423,25 @@
                 wait_frames(k, g + 1)
 
             acc = lax.fori_loop(
-                0, chunks, lambda c, a: chunk(k, g * chunks + c, a), acc, unroll=4
+                0, chunks, lambda c, a: chunk(k, g * chunks + c, a), acc, unroll=2
             )
             if k < ITERS - 1:
-                @pl.when(g < 1)
+                @pl.when(g < early)
                 def _():
                     send_frames(k + 1, g)
+
+                if relays:
+                    @pl.when(g >= relay_from)
+                    def _():
+                        send_relay(k + 1, g)
             return acc
 
         acc = lax.fori_loop(0, groups, group, jnp.zeros((8, 128), f32))
         next_hello(2 * k + 2)
         if k < ITERS - 1:
             send_small(k + 1)
-            for g in range(1, groups):
-                send_frames(k + 1, g)
+            for g in range(early, groups):
+                send_frames(k + 1, g, g < relay_from)
             acc = lax.fori_loop(
                 0, rows // 8, functools.partial(gap_chunk, k), acc, unroll=2
             )
@@ -420,6 +474,11 @@
             frame_out, 2, fs_sem.at[k],
             lambda c, k=k: ub[k].at[pl.ds(0, c), pl.ds(0, rows), pl.ds(0, cols)],
         )
+    for src, via, dst, i, slot in relays:
+        @pl.when(it == via)
+        def _(slot=slot):
+            sent = rbuf.at[slot]
+            pltpu.make_async_copy(sent, sent, fw_sem.at[slot]).wait()
     everything = grecv.at[pl.ds(0, n - 1)]
     pltpu.make_async_copy(everything, everything, gr_sem).wait()
     pltpu.make_async_copy(everything, everything, gs_sem).wait()
@@ -440,18 +499,39 @@
         c.wait()
 
 
+def corner_relays(mesh):
+    at = [getattr(d, "coords", None) for d in mesh.devices[:, 0, 0]]
+    relays, busy = [], {}
+    if any(c is None for c in at):
+        return relays
+    at = [tuple(c) for c in at]
+    for a in range(len(at) - 1):
+        for src, dst, i in ((a, a + 1, 1), (a + 1, a, 0)):
+            step = [abs(p - q) for p, q in zip(at[src], at[dst])]
+            corner = (at[src][0], at[dst][1], *at[src][2:])
+            if step == [1, 1, 0] and corner in at:
+                via = at.index(corner)
+                slot = busy[via] = busy.get(via, -1) + 1
+                relays.append((src, via, dst, i, slot))
+    return relays
+
+
 def solution(mesh):
     sizes = (mesh.shape["tm"], mesh.shape["row"], mesh.shape["col"])
     n = sizes[0] * sizes[1] * sizes[2]
+    relays = corner_relays(mesh)
+    slots = 1 + max([slot for *_, slot in relays], default=0)
 
     def on_device(noisy_video, fidelity):
         frames, rows, cols = noisy_video.shape
-        groups = 4
+        groups = 8
+        early = 4
+        held = groups // 2
         block = (frames, rows, cols)
         dma = pltpu.SemaphoreType.DMA
         vm = lambda *shape: pltpu.VMEM(shape, jnp.float32)
         outs = pl.pallas_call(
-            functools.partial(kernel, sizes, groups),
+            functools.partial(kernel, sizes, groups, early, relays),
             out_shape=(
                 pltpu.VMEM(block, jnp.float32),
                 pltpu.VMEM((ITERS,), jnp.float32),
@@ -478,6 +558,8 @@
                 dma((1,)), dma((ITERS,)), dma((1,)), dma((ITERS,)),
                 dma(()), dma(()),
                 pltpu.SemaphoreType.REGULAR((max(1, sum(sizes) - 4),)),
+                vm(slots, ITERS, held, rows // groups, cols),
+                dma((slots, ITERS, held)), dma((slots,)),
             ],
             compiler_params=pltpu.CompilerParams(
                 collective_id=0, has_side_effects=True

time: 34.3 us -> 32.2 us (0.939)
  Pallas kernels: 33.5 us -> 31.5 us
    pallas_call x1, Pallas kernels: 32.7 us -> 30.6 us  [on_device(): pl.pallas_call(functools.partial(kernel, sizes, groups, early, relays), o...]
where the time goes in v3:
time: 32.2 us; the launch traced here: 32.1 us
  Pallas kernels  31.5 us (98%)
  between operations  0.64 us (2%)
    pallas_call x1, Pallas kernels, on_device(): pl.pallas_call(functools.partial(kernel, sizes, groups, early, relays), o...  30.6 us
    pallas_call x1, Pallas kernels, on_device(): pl.pallas_call(put, out_shape=(jax.ShapeDtypeStruct(block, jnp.float32),...  0.81 us

profile of v3, /device:TPU:0, one launch (start us, length us, event | category | flops | bytes accessed | tf_op | source)
XLA Modules:
  0.0 32.1 jit_solution(1112133761788403714)
XLA Ops:
  0.6 30.6 %chambolle_pock.1 = (f32[4,128,256]{2,1,0:T(8,128)S(1)}, f32[3]{0:T(128)S(1)}) custom-call(f32[4,128,256]{2,1,0:T(8,128)} %f_hbm.1, f32[4,128,256]{2,1,0:T(8,128)} %lam_hbm.1), custom_call_target="tpu_custom_call" | custom-call | tf_op jit(solution)/shard_map/chambolle_pock/pallas_call | solution.py:533
  31.3 0.8 %put.1 = (f32[4,128,256]{2,1,0:T(8,128)}, f32[3]{0:T(128)}) custom-call(f32[4,128,256]{2,1,0:T(8,128)S(1)} %get-tuple-element.4.u, f32[3]{0:T(128)S(1)} %get-tuple-element.5.gaps), custom_call_target="tpu_custom_call" | custom-call | tf_op jit(solution)/shard_map/put/pallas_call | solution.py:569
